TPU v7x, 256 devices: a 2x2x32 block of a 4x8x32 slice. The times are simulated.
256 devices in a mesh: group: 4 (over y, x), blk: 64 (over z, core).
Axes of the slice: x: 2, y: 2, z: 32, core: 2. Of those that a mesh axis runs over, the one named last changes fastest.
The devices are a block of a 4x8x32 slice.
Arguments:
- queries: bfloat16 [8, 256, 2048], P('group', 'blk'), parts along dimension 0, may hold values from -160 to 160
- keys: bfloat16 [8, 81920, 256], P('group', 'blk'), parts along dimension 0, may hold values from -4 to 4
- values: bfloat16 [8, 81920, 256], P('group', 'blk'), parts along dimension 0, may hold values from -6 to 6
- lengths: int32 [8], P('group'), parts along dimension 0, may hold values from 61440 to 81920
- offsets: int32 [8], P('group'), parts along dimension 0, may hold values from 51200 to 81664
Outputs:
- attended: bfloat16 [8, 256, 2048], P('group', 'blk'), parts along dimension 0
There are 4 independent parts, one for each index of `group`. A program takes and returns all parts, laid end to end along the dimension named above; each array names one. Nothing has to cross between parts.
All inputs are finite; a program needn't handle non-finite values.
Results may differ from a plain program's by a relative error of at most 0.0085.
Values may be sent and summed in bfloat16 or wider, within the bound.
A program may use at most 64 MiB of HBM per device.

v0:
```python
import math
import jax
import jax.numpy as jnp
from jax import lax
from jax.sharding import PartitionSpec as P

KV_HEADS = 2
HEAD_DIM = 128
masked_low = -1e30


def shard_partial(query_rows, key_rows, value_rows, query_pos, key_pos, lengths):
    micro_count, rows_count, row_width = query_rows.shape
    heads_count = row_width // HEAD_DIM
    group_size = heads_count // KV_HEADS
    query_split = query_rows.reshape(micro_count, rows_count, KV_HEADS, group_size, HEAD_DIM)
    key_split = key_rows.reshape(micro_count, key_rows.shape[1], KV_HEADS, HEAD_DIM)
    value_split = value_rows.reshape(micro_count, value_rows.shape[1], KV_HEADS, HEAD_DIM)
    scores = jnp.einsum(
        "brkgd,bskd->bkgrs", query_split, key_split, preferred_element_type=jnp.float32
    )
    scores = scores * (1.0 / math.sqrt(HEAD_DIM))
    visible = (key_pos[None, None, :] <= query_pos[:, :, None]) & (
        key_pos[None, None, :] < lengths[:, None, None]
    )
    visible = visible[:, None, None, :, :]
    any_visible = jnp.any(visible, axis=-1)
    row_max = jnp.max(jnp.where(visible, scores, masked_low), axis=-1)
    safe_max = jnp.where(any_visible, row_max, 0.0)
    shifted = jnp.where(visible, scores - safe_max[..., None], 0.0)
    weights = jnp.where(visible, jnp.exp(shifted), 0.0)
    totals = jnp.sum(weights, axis=-1)
    bounded = jnp.maximum(totals, 1.0)
    numerator = jnp.einsum(
        "bkgrs,bskd->bkgrd",
        weights.astype(jnp.bfloat16),
        value_split,
        preferred_element_type=jnp.float32,
    )
    partial_value = (numerator / bounded[..., None]).astype(jnp.bfloat16)
    partial_value = jnp.transpose(partial_value, (0, 3, 1, 2, 4)).reshape(
        micro_count, rows_count, row_width
    )
    logsum = jnp.where(any_visible, safe_max + jnp.log(bounded), masked_low)
    logsum = jnp.transpose(logsum, (0, 3, 1, 2)).reshape(micro_count, rows_count, heads_count)
    return (partial_value, logsum)


def body(queries, keys, values, lengths, offsets):
    micro_count, local_rows, row_width = queries.shape
    local_keys = keys.shape[1]
    heads_count = row_width // HEAD_DIM
    shards = lax.axis_size("blk")
    key_pos = lax.axis_index("blk") * local_keys + jnp.arange(local_keys, dtype=jnp.int32)
    visiting = lax.all_gather(queries, "blk", axis=1, tiled=True)
    rows_count = visiting.shape[1]
    block_rows = math.gcd(rows_count, 64)
    block_count = rows_count // block_rows

    def one_block(block_index):
        block_start = block_index * block_rows
        selected = lax.dynamic_slice_in_dim(visiting, block_start, block_rows, 1)
        query_pos = (
            offsets[:, None] + block_start + jnp.arange(block_rows, dtype=jnp.int32)[None, :]
        )
        return shard_partial(selected, keys, values, query_pos, key_pos, lengths)

    block_parts, block_logs = lax.map(one_block, jnp.arange(block_count, dtype=jnp.int32))
    block_parts = jnp.moveaxis(block_parts, 0, 1).reshape(micro_count, rows_count, row_width)
    block_logs = jnp.moveaxis(block_logs, 0, 1).reshape(micro_count, rows_count, heads_count)
    partials = block_parts
    logsums = block_logs
    partials, logsums = (partials, logsums)
    shaped_parts = partials.reshape(micro_count, shards, local_rows, row_width)
    shaped_logs = logsums.reshape(micro_count, shards, local_rows, heads_count)
    home_parts = lax.all_to_all(shaped_parts, "blk", split_axis=1, concat_axis=1, tiled=True)
    home_logs = lax.all_to_all(shaped_logs, "blk", split_axis=1, concat_axis=1, tiled=True)
    row_peak = jnp.max(home_logs, axis=1, keepdims=True)
    scales = jnp.exp(home_logs - row_peak)
    denominator = jnp.sum(scales, axis=1)
    split_parts = home_parts.reshape(micro_count, shards, local_rows, heads_count, HEAD_DIM)
    weighted = jnp.sum(split_parts * scales[..., None], axis=1)
    merged = weighted / denominator[..., None]
    attended = merged.reshape(micro_count, local_rows, row_width).astype(jnp.bfloat16)
    return attended


def solution(mesh):
    return jax.shard_map(
        body,
        mesh=mesh,
        in_specs=(
            P("group", "blk", None),
            P("group", "blk", None),
            P("group", "blk", None),
            P("group"),
            P("group"),
        ),
        out_specs=P("group", "blk", None),
        check_vma=False,
    )
```

profile of v0, /device:TPU:37, one launch (start us, length us, event | category | flops | bytes accessed | tf_op | source)
XLA Modules:
  0.0 481.0 jit_solution(16185152529671269494)
XLA Ops:
  6.6 1.4 copy.51
  8.1 3.8 reshape.97
  11.9 2.9 reshape.98
  14.9 139.4 %all-gather.2.cloned.1.call-done = bf16[2,256,2048]{2,0,1:T(2,128)(2,1)} async-done(((bf16[2,4,2048]{2,0,1:T(2,128)(2,1)}), bf16[2,256,2048]{2,0,1:T(2,128)(2,1)}) %all-gather.2.cloned.1.call-update) | async-done | bytes 2097168 | tf_op jit(solution)/shard_map/all_gather | solution.py:55
  154.3 71.4 %while.14 = (s32[]{:T(128)}, bf16[4,2,64,2048]{3,2,1,0:T(8,128)(2,1)}, f32[4,2,64,16]{2,3,1,0:T(8,128)S(1)}, s32[4]{0:T(128)S(1)}, s32[2]{0:T(128)S(1)}, /*index...) while((s32[]{:T(128)}, ...), condition=%wide.wide.region_4.5_spmd.clone, body=%wide.wide.region_0.4_spmd.clone.sunk | while | flops 1377611520 | bytes 88389816 | solution.py:68
  154.3 0.6 dynamic_slice.15
  155.5 1.4 constant_dynamic-slice_fusion.3
  156.9 0.3 reshape.103
  157.6 3.0 fusion.38
  160.6 0.3 and_reduce_fusion.3
  161.0 4.3 fusion.39
  165.5 5.4 %divide_convert_fusion.4 = bf16[2,64,2,8,128]{4,3,1,2,0:T(8,128)(2,1)S(1)} fusion(bf16[2,1280,2,128,1]{3,2,1,0,4:T(2,128)(2,1)S(1)} %bitcast.95, f32[2,2,64,8,1280]{4,3,2,1,0:T(8,128)} %copy-done, f32[2,2,8,64]{2,3,1,0:T(8,128)S(1)} %broadcast_select_fusion.3, pred[2,64,1280]{2,1,0:T(8,128)(4,1)S(1)} %compare_and_fusion.3, ...), kind=kOutput, calls=%fused_computation.15.clone.clone.1 | convolution fusion | flops 684720128 | bytes 12500992 | tf_op jit(solution)/shard_map/while/body/eval_jaxpr/bkgrs,bskd->bkgrd/dot_general | solution.py:34
  171.3 0.9 constant_dynamic-update-slice_fusion.3
  172.1 0.6 dynamic_slice.15
  173.4 1.4 constant_dynamic-slice_fusion.3
  174.8 0.3 reshape.103
  175.5 3.0 fusion.38
  178.5 0.3 and_reduce_fusion.3
  178.8 4.3 fusion.39
  183.4 5.4 %divide_convert_fusion.4 = bf16[2,64,2,8,128]{4,3,1,2,0:T(8,128)(2,1)S(1)} fusion(bf16[2,1280,2,128,1]{3,2,1,0,4:T(2,128)(2,1)S(1)} %bitcast.95, f32[2,2,64,8,1280]{4,3,2,1,0:T(8,128)} %copy-done, f32[2,2,8,64]{2,3,1,0:T(8,128)S(1)} %broadcast_select_fusion.3, pred[2,64,1280]{2,1,0:T(8,128)(4,1)S(1)} %compare_and_fusion.3, ...), kind=kOutput, calls=%fused_computation.15.clone.clone.1 | convolution fusion | flops 684720128 | bytes 12500992 | tf_op jit(solution)/shard_map/while/body/eval_jaxpr/bkgrs,bskd->bkgrd/dot_general | solution.py:34
  189.1 0.9 constant_dynamic-update-slice_fusion.3
  190.0 0.6 dynamic_slice.15
  191.3 1.4 constant_dynamic-slice_fusion.3
  192.7 0.3 reshape.103
  193.4 3.0 fusion.38
  196.3 0.3 and_reduce_fusion.3
  196.7 4.3 fusion.39
  201.3 5.4 %divide_convert_fusion.4 = bf16[2,64,2,8,128]{4,3,1,2,0:T(8,128)(2,1)S(1)} fusion(bf16[2,1280,2,128,1]{3,2,1,0,4:T(2,128)(2,1)S(1)} %bitcast.95, f32[2,2,64,8,1280]{4,3,2,1,0:T(8,128)} %copy-done, f32[2,2,8,64]{2,3,1,0:T(8,128)S(1)} %broadcast_select_fusion.3, pred[2,64,1280]{2,1,0:T(8,128)(4,1)S(1)} %compare_and_fusion.3, ...), kind=kOutput, calls=%fused_computation.15.clone.clone.1 | convolution fusion | flops 684720128 | bytes 12500992 | tf_op jit(solution)/shard_map/while/body/eval_jaxpr/bkgrs,bskd->bkgrd/dot_general | solution.py:34
  207.0 0.8 constant_dynamic-update-slice_fusion.3
  207.8 0.6 dynamic_slice.15
  209.1 1.4 constant_dynamic-slice_fusion.3
  210.5 0.3 reshape.103
  211.2 3.0 fusion.38
  214.5 4.3 fusion.39
  219.1 5.4 %divide_convert_fusion.4 = bf16[2,64,2,8,128]{4,3,1,2,0:T(8,128)(2,1)S(1)} fusion(bf16[2,1280,2,128,1]{3,2,1,0,4:T(2,128)(2,1)S(1)} %bitcast.95, f32[2,2,64,8,1280]{4,3,2,1,0:T(8,128)} %copy-done, f32[2,2,8,64]{2,3,1,0:T(8,128)S(1)} %broadcast_select_fusion.3, pred[2,64,1280]{2,1,0:T(8,128)(4,1)S(1)} %compare_and_fusion.3, ...), kind=kOutput, calls=%fused_computation.15.clone.clone.1 | convolution fusion | flops 684720128 | bytes 12500992 | tf_op jit(solution)/shard_map/while/body/eval_jaxpr/bkgrs,bskd->bkgrd/dot_general | solution.py:34
  224.8 0.8 constant_dynamic-update-slice_fusion.3
  225.9 0.8 reshape.95
  226.7 13.8 %all-to-all-start.1 = ((f32[64,1,128]{2,1,0:T(1,128)}), f32[64,1,128]{2,1,0:T(1,128)S(1)}, u32[]{:S(2)}, u32[]{:S(2)}) async-start(f32[64,1,128]{2,1,0:T(1,128)} %reshape.95), calls=%async_computation.1 | async-start | bytes 65536 | tf_op jit(solution)/shard_map/all_to_all | solution.py:77
  240.5 5.1 %copy.53 = bf16[2,4,64,2048]{3,0,2,1:T(2,128)(2,1)} copy(bf16[2,4,64,2048]{3,2,0,1:T(8,128)(2,1)} %bitcast.94) | data formatting | bytes 4194304 | tf_op jit(solution)/shard_map/transpose | solution.py:69
  245.6 16.6 %all-to-all-done.1 = f32[64,1,128]{2,1,0:T(1,128)S(1)} async-done(((f32[64,1,128]{2,1,0:T(1,128)}), f32[64,1,128]{2,1,0:T(1,128)S(1)}, u32[]{:S(2)}, u32[]{:S(2)}) %all-to-all-start.1) | async-done | bytes 32800 | tf_op jit(solution)/shard_map/all_to_all | solution.py:77
  262.2 6.6 %all-to-all-start = ((bf16[2,64,4,2048]{3,0,2,1:T(2,128)(2,1)}), bf16[2,64,4,2048]{3,0,2,1:T(2,128)(2,1)S(1)}, u32[]{:S(2)}, u32[]{:S(2)}) async-start(bf16[2,64,4,2048]{3,0,2,1:T(2,128)(2,1)} %bitcast.93), calls=%async_computation | async-start | bytes 4194304 | tf_op jit(solution)/shard_map/all_to_all | solution.py:76
  268.8 0.5 broadcast.111
  269.4 0.7 reduce.2
  270.7 2.6 mul.27
  273.3 5.8 %mul.28 = f32[2,64,4,2048]{3,0,2,1:T(2,128)} reshape(f32[2,64,4,16,128]{4,3,0,2,1:T(8,128)} %mul.27) | data formatting | bytes 8388608 | tf_op jit(solution)/shard_map/mul | solution.py:82
  279.2 189.7 %all-to-all-done = bf16[2,64,4,2048]{3,0,2,1:T(2,128)(2,1)S(1)} async-done(((bf16[2,64,4,2048]{3,0,2,1:T(2,128)(2,1)}), bf16[2,64,4,2048]{3,0,2,1:T(2,128)(2,1)S(1)}, u32[]{:S(2)}, u32[]{:S(2)}) %all-to-all-start) | async-done | bytes 2097184 | tf_op jit(solution)/shard_map/all_to_all | solution.py:76
  468.9 4.5 multiply_reduce_fusion
  473.5 0.6 copy.58
  (84 shorter events, 5.0 us)
Async XLA Ops:
  6.5 147.7 %copy-start.2 = (s32[2]{0:T(128)S(1)}, s32[2]{0:T(128)}, u32[]{:S(2)}) copy-start(s32[2]{0:T(128)} %param.10) | copy-start | bytes 28
  6.5 147.7 %copy-start.3 = (s32[2]{0:T(128)S(1)}, s32[2]{0:T(128)}, u32[]{:S(2)}) copy-start(s32[2]{0:T(128)} %param.11) | copy-start | bytes 28
  6.6 147.7 %all-gather.2.cloned.1.call-start = ((), (), s32[]{:S(2)}) async-start(), calls=%async_computation.2 | async-start | bytes 2129920 | tf_op jit(solution)/shard_map/all_gather | solution.py:55
  160.6 4.7 copy-start
  161.0 4.5 copy-start.1
  178.5 4.7 copy-start
  178.8 4.5 copy-start.1
  196.3 4.7 copy-start
  196.7 4.5 copy-start.1
  214.2 4.7 copy-start
  214.5 4.5 copy-start.1
  226.7 35.6 %all-to-all-start.1 = ((f32[64,1,128]{2,1,0:T(1,128)}), f32[64,1,128]{2,1,0:T(1,128)S(1)}, u32[]{:S(2)}, u32[]{:S(2)}) async-start(f32[64,1,128]{2,1,0:T(1,128)} %reshape.95), calls=%async_computation.1 | async-start | bytes 65536 | tf_op jit(solution)/shard_map/all_to_all | solution.py:77
  262.2 206.7 %all-to-all-start = ((bf16[2,64,4,2048]{3,0,2,1:T(2,128)(2,1)}), bf16[2,64,4,2048]{3,0,2,1:T(2,128)(2,1)S(1)}, u32[]{:S(2)}, u32[]{:S(2)}) async-start(bf16[2,64,4,2048]{3,0,2,1:T(2,128)(2,1)} %bitcast.93), calls=%async_computation | async-start | bytes 4194304 | tf_op jit(solution)/shard_map/all_to_all | solution.py:76
Sparse Core Ops, SparseCore 0:
  9.2 145.0 all-gather.1
where the time goes:
time: 482 us; the launch traced here: 481 us
  waiting for transfers between devices  346 us (72%)
  local copies, waits for them, and re-layouts  38.7 us (8%)
  matrix products  33.6 us (7%)
  other arithmetic  26 us (5%)
  starting transfers between devices  20.4 us (4%)
  between operations  13.5 us (3%)
    all_to_all x1, waiting for transfers between devices, body(): lax.all_to_all(shaped_parts, 'blk', split_axis=1, concat_axis=1, tiled=True)  190 us
    all_gather x1, waiting for transfers between devices, body(): visiting = lax.all_gather(queries, 'blk', axis=1, tiled=True)  139 us
    dot_general x4, matrix products, shard_partial(): jnp.einsum('bkgrs,bskd->bkgrd', weights.astype(jnp.bfloat16), value_split...  21.7 us
    reduce_sum x4, other arithmetic, shard_partial(): totals = jnp.sum(weights, axis=-1)  17.2 us
    all_to_all x1, waiting for transfers between devices, body(): lax.all_to_all(shaped_logs, 'blk', split_axis=1, concat_axis=1, tiled=True)  16.6 us
    all_to_all x1, starting transfers between devices, body(): lax.all_to_all(shaped_logs, 'blk', split_axis=1, concat_axis=1, tiled=True)  13.8 us
    dot_general x4, matrix products, shard_partial(): jnp.einsum('brkgd,bskd->bkgrs', query_split, key_split, preferred_element...  11.8 us
  transfers between devices with their start and end apart: 3, of which 3 were waited for; matrix products, arithmetic and copies ran while one was open for 5% of the time, Pallas kernels for 0%

commit v1 on v0

--- a/solution.py
+++ b/solution.py
@@ -52,7 +52,11 @@
     heads_count = row_width // HEAD_DIM
     shards = lax.axis_size("blk")
     key_pos = lax.axis_index("blk") * local_keys + jnp.arange(local_keys, dtype=jnp.int32)
-    visiting = lax.all_gather(queries, "blk", axis=1, tiled=True)
+    peers = lax.axis_size("blk")
+    repeats = [peers if d == 1 else 1 for d in range(queries.ndim)]
+    visiting = lax.all_to_all(
+        jnp.tile(queries, repeats), "blk", split_axis=1, concat_axis=1, tiled=True
+    )
     rows_count = visiting.shape[1]
     block_rows = math.gcd(rows_count, 64)
     block_count = rows_count // block_rows

time: 482 us -> 551 us (1.14)
  waiting for transfers between devices: 346 us -> 401 us
  starting transfers between devices: 20.4 us -> 48.3 us
  between operations: 13.5 us -> 0.14 us
    all_to_all x0 -> x1, waiting for transfers between devices: none -> 196 us  [body(): lax.all_to_all(jnp.tile(queries, repeats), 'blk', split_axis=1, concat_ax...]
    all_gather x1 -> x0, waiting for transfers between devices: 139 us -> none  [body(): visiting = lax.all_gather(queries, 'blk', axis=1, tiled=True)]
    all_to_all x0 -> x1, starting transfers between devices: none -> 34.5 us  [body(): lax.all_to_all(jnp.tile(queries, repeats), 'blk', split_axis=1, concat_ax...]
    all_to_all x1, starting transfers between devices: 13.8 us -> 7.82 us  [body(): lax.all_to_all(shaped_logs, 'blk', split_axis=1, concat_axis=1, tiled=True)]
  transfers between devices with their start and end apart: 3 -> 3, of which waited for: 3 -> 3; matrix products, arithmetic and copies ran while one was open for 5% -> 3% of each run, Pallas kernels for 0% -> 0%
where the time goes in v1:
time: 551 us; the launch traced here: 549 us
  waiting for transfers between devices  401 us (73%)
  starting transfers between devices  48.3 us (9%)
  local copies, waits for them, and re-layouts  36.6 us (7%)
  matrix products  33.5 us (6%)
  other arithmetic  26 us (5%)
    all_to_all x1, waiting for transfers between devices, body(): lax.all_to_all(jnp.tile(queries, repeats), 'blk', split_axis=1, concat_ax...  196 us
    all_to_all x1, waiting for transfers between devices, body(): lax.all_to_all(shaped_parts, 'blk', split_axis=1, concat_axis=1, tiled=True)  187 us
    all_to_all x1, starting transfers between devices, body(): lax.all_to_all(jnp.tile(queries, repeats), 'blk', split_axis=1, concat_ax...  34.5 us
    dot_general x4, matrix products, shard_partial(): jnp.einsum('bkgrs,bskd->bkgrd', weights.astype(jnp.bfloat16), value_split...  21.7 us
    all_to_all x1, waiting for transfers between devices, body(): lax.all_to_all(shaped_logs, 'blk', split_axis=1, concat_axis=1, tiled=True)  17.5 us
    reduce_sum x4, other arithmetic, shard_partial(): totals = jnp.sum(weights, axis=-1)  17.2 us
    dot_general x4, matrix products, shard_partial(): jnp.einsum('brkgd,bskd->bkgrs', query_split, key_split, preferred_element...  11.8 us
  transfers between devices with their start and end apart: 3, of which 3 were waited for; matrix products, arithmetic and copies ran while one was open for 3% of the time, Pallas kernels for 0%

profile of v1, /device:TPU:37, one launch (start us, length us, event | category | flops | bytes accessed | tf_op | source)
XLA Modules:
  0.0 548.6 jit_solution(2496622524709183026)
XLA Ops:
  0.0 0.9 copy.51
  0.9 3.4 tile.4
  4.3 34.5 %all-to-all-start = ((bf16[2,256,2048]{2,0,1:T(2,128)(2,1)}), bf16[2,256,2048]{2,0,1:T(2,128)(2,1)}, u32[]{:S(2)}, u32[]{:S(2)}) async-start(bf16[2,256,2048]{2,0,1:T(2,128)(2,1)} %bitcast), calls=%async_computation | async-start | bytes 4194304 | tf_op jit(solution)/shard_map/all_to_all | solution.py:57
  38.8 1.2 reshape.101
  40.1 0.3 reshape.102
  40.4 195.8 %all-to-all-done = bf16[2,256,2048]{2,0,1:T(2,128)(2,1)} async-done(((bf16[2,256,2048]{2,0,1:T(2,128)(2,1)}), bf16[2,256,2048]{2,0,1:T(2,128)(2,1)}, u32[]{:S(2)}, u32[]{:S(2)}) %all-to-all-start) | async-done | bytes 2097184 | tf_op jit(solution)/shard_map/all_to_all | solution.py:57
  236.2 71.9 %while.14 = (s32[]{:T(128)}, bf16[4,2,64,2048]{3,2,1,0:T(8,128)(2,1)}, f32[4,2,64,16]{2,3,1,0:T(8,128)S(1)}, s32[4]{0:T(128)S(1)}, s32[2]{0:T(128)S(1)}, /*index...) while((s32[]{:T(128)}, ...), condition=%wide.wide.region_4.5_spmd.clone, body=%wide.wide.region_0.4_spmd.clone.sunk | while | flops 1377611520 | bytes 88389816 | solution.py:72
  236.3 0.7 dynamic_slice.15
  237.6 1.4 constant_dynamic-slice_fusion.3
  239.0 0.3 reshape.107
  239.7 3.0 fusion.38
  242.7 0.3 and_reduce_fusion.3
  243.1 4.3 fusion.39
  247.6 5.4 divide_convert_fusion.4
  253.4 0.9 constant_dynamic-update-slice_fusion.3
  254.2 0.7 dynamic_slice.15
  255.6 1.4 constant_dynamic-slice_fusion.3
  257.0 0.3 reshape.107
  257.7 3.0 fusion.38
  261.0 4.3 fusion.39
  265.6 5.4 divide_convert_fusion.4
  271.4 0.9 constant_dynamic-update-slice_fusion.3
  272.2 0.7 dynamic_slice.15
  273.6 1.4 constant_dynamic-slice_fusion.3
  275.0 0.3 reshape.107
  275.7 3.0 fusion.38
  279.0 4.3 fusion.39
  283.6 5.4 divide_convert_fusion.4
  289.3 0.8 constant_dynamic-update-slice_fusion.3
  290.2 0.7 dynamic_slice.15
  291.5 1.4 constant_dynamic-slice_fusion.3
  292.9 0.3 reshape.107
  293.6 3.0 fusion.38
  297.0 4.3 fusion.39
  301.5 5.4 divide_convert_fusion.4
  307.3 0.8 constant_dynamic-update-slice_fusion.3
  308.3 0.8 reshape.99
  309.1 7.8 %all-to-all-start.2 = ((f32[64,1,128]{2,1,0:T(1,128)}), f32[64,1,128]{2,1,0:T(1,128)S(1)}, u32[]{:S(2)}, u32[]{:S(2)}) async-start(f32[64,1,128]{2,1,0:T(1,128)} %reshape.99), calls=%async_computation.2 | async-start | bytes 65536 | tf_op jit(solution)/shard_map/all_to_all | solution.py:81
  317.0 5.1 copy.53
  322.1 17.5 %all-to-all-done.2 = f32[64,1,128]{2,1,0:T(1,128)S(1)} async-done(((f32[64,1,128]{2,1,0:T(1,128)}), f32[64,1,128]{2,1,0:T(1,128)S(1)}, u32[]{:S(2)}, u32[]{:S(2)}) %all-to-all-start.2) | async-done | bytes 32800 | tf_op jit(solution)/shard_map/all_to_all | solution.py:81
  339.6 6.0 %all-to-all-start.1 = ((bf16[2,64,4,2048]{3,0,2,1:T(2,128)(2,1)}), bf16[2,64,4,2048]{3,0,2,1:T(2,128)(2,1)S(1)}, u32[]{:S(2)}, u32[]{:S(2)}) async-start(bf16[2,64,4,2048]{3,0,2,1:T(2,128)(2,1)} %bitcast.94), calls=%async_computation.1 | async-start | bytes 4194304 | tf_op jit(solution)/shard_map/all_to_all | solution.py:80
  345.7 0.5 broadcast.114
  346.2 0.7 reduce.2
  347.5 2.6 mul.27
  350.1 5.8 %mul.28 = f32[2,64,4,2048]{3,0,2,1:T(2,128)} reshape(f32[2,64,4,16,128]{4,3,0,2,1:T(8,128)} %mul.27) | data formatting | bytes 8388608 | tf_op jit(solution)/shard_map/mul | solution.py:86
  356.0 187.4 %all-to-all-done.1 = bf16[2,64,4,2048]{3,0,2,1:T(2,128)(2,1)S(1)} async-done(((bf16[2,64,4,2048]{3,0,2,1:T(2,128)(2,1)}), bf16[2,64,4,2048]{3,0,2,1:T(2,128)(2,1)S(1)}, u32[]{:S(2)}, u32[]{:S(2)}) %all-to-all-start.1) | async-done | bytes 2097184 | tf_op jit(solution)/shard_map/all_to_all | solution.py:80
  543.4 4.5 multiply_reduce_fusion
  548.0 0.6 copy.58
  (88 shorter events, 5.5 us)
Async XLA Ops:
  0.0 38.8 %copy-start.2 = (bf16[2,1280,256]{2,1,0:T(8,128)(2,1)S(1)}, bf16[2,1280,256]{2,1,0:T(8,128)(2,1)}, u32[]{:S(2)}) copy-start(bf16[2,1280,256]{2,1,0:T(8,128)(2,1)} %param.9) | copy-start | bytes 3932164
  0.9 39.2 %copy-start.1 = (bf16[2,1280,256]{2,1,0:T(8,128)(2,1)S(1)}, bf16[2,1280,256]{2,1,0:T(8,128)(2,1)}, u32[]{:S(2)}) copy-start(bf16[2,1280,256]{2,1,0:T(8,128)(2,1)} %param.8) | copy-start | bytes 3932164
  4.3 232.0 %copy-start.4 = (s32[2]{0:T(128)S(1)}, s32[2]{0:T(128)}, u32[]{:S(2)}) copy-start(s32[2]{0:T(128)} %param.10) | copy-start | bytes 28
  4.3 232.0 %copy-start.5 = (s32[2]{0:T(128)S(1)}, s32[2]{0:T(128)}, u32[]{:S(2)}) copy-start(s32[2]{0:T(128)} %param.11) | copy-start | bytes 28
  4.3 231.9 %all-to-all-start = ((bf16[2,256,2048]{2,0,1:T(2,128)(2,1)}), bf16[2,256,2048]{2,0,1:T(2,128)(2,1)}, u32[]{:S(2)}, u32[]{:S(2)}) async-start(bf16[2,256,2048]{2,0,1:T(2,128)(2,1)} %bitcast), calls=%async_computation | async-start | bytes 4194304 | tf_op jit(solution)/shard_map/all_to_all | solution.py:57
  242.7 4.7 copy-start
  243.1 4.5 copy-start.3
  260.7 4.7 copy-start
  261.0 4.5 copy-start.3
  278.7 4.7 copy-start
  279.0 4.5 copy-start.3
  296.6 4.7 copy-start
  297.0 4.5 copy-start.3
  309.1 30.5 %all-to-all-start.2 = ((f32[64,1,128]{2,1,0:T(1,128)}), f32[64,1,128]{2,1,0:T(1,128)S(1)}, u32[]{:S(2)}, u32[]{:S(2)}) async-start(f32[64,1,128]{2,1,0:T(1,128)} %reshape.99), calls=%async_computation.2 | async-start | bytes 65536 | tf_op jit(solution)/shard_map/all_to_all | solution.py:81
  339.6 203.8 %all-to-all-start.1 = ((bf16[2,64,4,2048]{3,0,2,1:T(2,128)(2,1)}), bf16[2,64,4,2048]{3,0,2,1:T(2,128)(2,1)S(1)}, u32[]{:S(2)}, u32[]{:S(2)}) async-start(bf16[2,64,4,2048]{3,0,2,1:T(2,128)(2,1)} %bitcast.94), calls=%async_computation.1 | async-start | bytes 4194304 | tf_op jit(solution)/shard_map/all_to_all | solution.py:80
